TPU v7x, 32 devices: a whole 2x2x4 slice. The times are simulated.
32 devices in a mesh: section: 4 (over y, x), dev: 8 (over z, core).
Axes of the slice: x: 2, y: 2, z: 4, core: 2. Of those that a mesh axis runs over, the one named last changes fastest.
Arguments:
- late_sent: bfloat16 [4, 784, 1024], P('section', 'dev'), may hold values from -5 to 5
- entry_rows: bfloat16 [784, 1024], P('dev'), may hold values from -5 to 5
- gain_first: float32 [4, 1024], P('section'), may hold values from 0.1 to 1.9
- shift_first: float32 [4, 1024], P('section'), may hold values from -3 to 3
- expand_late: bfloat16 [4, 1024, 4096], P('section', None, 'dev'), may hold values from -0.1875 to 0.1875
- gain_inner: float32 [4, 4096], P('section', 'dev'), may hold values from 0.1 to 1.9
- shift_inner: float32 [4, 4096], P('section', 'dev'), may hold values from -3 to 3
- reduce_late: bfloat16 [4, 4096, 1024], P('section', 'dev'), may hold values from -0.09375 to 0.09375
- early_saved: bfloat16 [4, 12544, 256], P('section', 'dev'), may hold values from -6 to 6
- upstream_grad: bfloat16 [4, 12544, 256], P('section', 'dev'), may hold values from -6 to 6
- exit_grad: bfloat16 [12544, 256], P('dev'), may hold values from -6 to 6
- expand_early: bfloat16 [4, 256, 1024], P('section'), may hold values from -0.375 to 0.375
- reduce_early: bfloat16 [4, 1024, 256], P('section'), may hold values from -0.1875 to 0.1875
Outputs:
- late_out: bfloat16 [4, 784, 1024], P('section', 'dev')
- input_grad: bfloat16 [4, 12544, 256], P('section', 'dev')
- grad_expand: float32 [4, 256, 1024], P('section')
- grad_reduce: float32 [4, 1024, 256], P('section')
All inputs are finite; a program needn't handle non-finite values.
Results may differ from a plain program's by a relative error of at most 0.02.
Values may be sent and summed in bfloat16 or wider, within the bound.
A program may use at most 128 MiB of HBM per device.

v0:
```python
import math

import jax
import jax.numpy as jnp
from jax import lax
from jax.sharding import PartitionSpec as P

epsilon = 1e-05


def from_behind(x, axis, by):
    peers = lax.axis_size(axis)
    pairs = [(i, i + by) for i in range(peers) if 0 <= i + by < peers]
    return lax.ppermute(x, axis, pairs)


def affine(sums, squares, count, gain, shift):
    average = sums / count
    second = squares / count
    spread = gain * lax.rsqrt(second - average * average + epsilon)
    return (spread, shift - average * spread)


def silu_slope(values):
    sigma = jax.nn.sigmoid(values)
    return sigma * (1.0 + values * (1.0 - sigma))


def late_part(
    late_sent,
    entry_rows,
    gain_first,
    shift_first,
    expand_late,
    gain_inner,
    shift_inner,
    reduce_late,
):
    section_index = lax.axis_index("section")
    rows_dev = entry_rows.shape[0]
    total_rows = rows_dev * lax.axis_size("dev")
    expand = expand_late[0]
    arrived = from_behind(late_sent[0], "section", 1)
    own_rows = jnp.where(section_index == 0, entry_rows, arrived)
    values = own_rows.astype(jnp.float32)
    sums, squares = lax.psum((jnp.sum(values, axis=0), jnp.sum(values * values, axis=0)), "dev")
    spread, offset = affine(sums, squares, total_rows, gain_first[0], shift_first[0])
    first = jax.nn.silu(
        lax.all_gather(own_rows, "dev", axis=0, tiled=True).astype(jnp.float32) * spread + offset
    ).astype(jnp.bfloat16)
    inner = jnp.dot(first, expand, preferred_element_type=jnp.float32)
    spread_two, offset_two = affine(
        jnp.sum(inner, axis=0),
        jnp.sum(inner * inner, axis=0),
        total_rows,
        gain_inner[0],
        shift_inner[0],
    )
    hidden = jax.nn.silu(inner * spread_two + offset_two).astype(jnp.bfloat16)
    reduce_weight = reduce_late[0]
    summed = lax.psum_scatter(
        jnp.dot(hidden, reduce_weight, preferred_element_type=jnp.float32).astype(jnp.bfloat16),
        "dev",
        scatter_dimension=0,
        tiled=True,
    ).astype(jnp.float32)
    return (own_rows.astype(jnp.float32) + summed).astype(jnp.bfloat16)[None]


def early_part(early_saved, upstream_grad, exit_grad, expand_early, reduce_early):
    section_index = lax.axis_index("section")
    arrived = from_behind(upstream_grad[0], "section", -1)
    grad = jnp.where(section_index == lax.axis_size("section") - 1, exit_grad, arrived)
    saved = early_saved[0]
    expand = expand_early[0]
    reduce_weight = reduce_early[0]
    pre = jnp.dot(saved, expand, preferred_element_type=jnp.float32)
    hidden = jax.nn.silu(pre).astype(jnp.bfloat16)
    back = lax.dot_general(
        grad, reduce_weight, (((1,), (1,)), ((), ())), preferred_element_type=jnp.float32
    )
    slope = (back * silu_slope(pre)).astype(jnp.bfloat16)
    local_expand = lax.dot_general(
        saved, slope, (((0,), (0,)), ((), ())), preferred_element_type=jnp.float32
    )
    local_reduce = lax.dot_general(
        hidden, grad, (((0,), (0,)), ((), ())), preferred_element_type=jnp.float32
    )
    summed_expand, summed_reduce = lax.psum((local_expand, local_reduce), "dev")
    result = grad.astype(jnp.float32) + lax.dot_general(
        slope, expand, (((1,), (1,)), ((), ())), preferred_element_type=jnp.float32
    )
    factor = 1.0 / math.sqrt(saved.shape[0] * lax.axis_size("dev"))
    return (
        result.astype(jnp.bfloat16)[None],
        (summed_expand * factor)[None],
        (summed_reduce * factor)[None],
    )


def shards(
    late_sent,
    entry_rows,
    gain_first,
    shift_first,
    expand_late,
    gain_inner,
    shift_inner,
    reduce_late,
    early_saved,
    upstream_grad,
    exit_grad,
    expand_early,
    reduce_early,
):
    late_out = late_part(
        late_sent,
        entry_rows,
        gain_first,
        shift_first,
        expand_late,
        gain_inner,
        shift_inner,
        reduce_late,
    )
    input_grad, grad_expand, grad_reduce = early_part(
        early_saved, upstream_grad, exit_grad, expand_early, reduce_early
    )
    return (late_out, input_grad, grad_expand, grad_reduce)


def solution(mesh):
    in_specs = (
        P("section", "dev", None),
        P("dev", None),
        P("section", None),
        P("section", None),
        P("section", None, "dev"),
        P("section", "dev"),
        P("section", "dev"),
        P("section", "dev", None),
        P("section", "dev", None),
        P("section", "dev", None),
        P("dev", None),
        P("section", None, None),
        P("section", None, None),
    )
    out_specs = (
        P("section", "dev", None),
        P("section", "dev", None),
        P("section", None, None),
        P("section", None, None),
    )
    return jax.shard_map(shards, mesh=mesh, in_specs=in_specs, out_specs=out_specs, check_vma=False)
```

profile of v0, /device:TPU:5, one launch (start us, length us, event | category | flops | bytes accessed | tf_op | source)
XLA Modules:
  0.0 179.0 jit_solution(4073630690061553025)
XLA Ops:
  7.2 3.2 %collective-permute-start.1 = (bf16[1568,256]{1,0:T(8,128)(2,1)}, bf16[1568,256]{1,0:T(8,128)(2,1)S(1)}, u32[]{:S(2)}, u32[]{:S(2)}) collective-permute-start(bf16[1568,256]{1,0:T(8,128)(2,1)} %bitcast.56), channel_id=1, source_target_pairs={{8,0},{16,8},{24,16},{9,1},{17,9},{25,17},{10,2},{18,10},{26,18},{... | collective-permute-start | bytes 2408456 | tf_op jit(solution)/shard_map/ppermute | solution.py:14
  10.4 2.4 %fusion.7 = f32[1568,1024]{1,0:T(8,128)S(1)} fusion(bf16[1,1568,256]{2,1,0:T(8,128)(2,1)} %param.21, bf16[1,256,1024]{2,1,0:T(8,128)(2,1)} %param.24), kind=kOutput, calls=%fused_computation.17 | convolution fusion | flops 822083584 | bytes 7749632 | tf_op jit(solution)/shard_map/dot_general | solution.py:77
  12.8 15.4 %collective-permute-done.1 = bf16[1568,256]{1,0:T(8,128)(2,1)S(1)} collective-permute-done((bf16[1568,256]{1,0:T(8,128)(2,1)}, bf16[1568,256]{1,0:T(8,128)(2,1)S(1)}, u32[]{:S(2)}, u32[]{:S(2)}) %collective-permute-start.1) | collective-permute-done | bytes 802848 | tf_op jit(solution)/shard_map/ppermute | solution.py:14
  28.4 2.8 %fusion.1 = f32[1024,256]{1,0:T(8,128)} fusion(bf16[1568,256]{1,0:T(8,128)(2,1)S(1)} %broadcast_select_fusion, f32[1568,1024]{1,0:T(8,128)S(1)} %fusion.7), kind=kOutput, calls=%fused_computation.4 | convolution fusion | flops 830111744 | bytes 8273920 | tf_op jit(solution)/shard_map/dot_general | solution.py:86
  31.2 2.7 %multiply_convert_fusion.1 = bf16[1568,1024]{1,0:T(8,128)(2,1)S(1)} fusion(f32[1568,1024]{1,0:T(8,128)S(1)} %fusion.7, bf16[1568,256]{1,0:T(8,128)(2,1)S(1)} %broadcast_select_fusion, bf16[1,1024,256]{2,1,0:T(8,128)(2,1)S(1)} %copy-done.12), kind=kOutput, calls=%fused_computation.1 | convolution fusion | flops 836534272 | bytes 10960896 | tf_op jit(solution)/shard_map/dot_general | solution.py:79
  34.0 1.7 copy-done.14
  35.7 2.1 %convolution_bitcast_fusion = f32[256,1024]{0,1:T(8,128)} fusion(bf16[1568,1024]{1,0:T(8,128)(2,1)S(1)} %multiply_convert_fusion.1, bf16[1,1568,256]{2,1,0:T(8,128)(2,1)S(1)} %copy-done.2), kind=kOutput, calls=%fused_computation.10 | convolution fusion | flops 822083584 | bytes 5062656 | tf_op jit(solution)/shard_map/dot_general | solution.py:83
  37.9 1.9 %collective-permute-start = (bf16[98,1024]{1,0:T(8,128)(2,1)S(1)}, bf16[98,1024]{1,0:T(8,128)(2,1)S(1)}, u32[]{:S(2)}, u32[]{:S(2)}) collective-permute-start(bf16[98,1024]{1,0:T(8,128)(2,1)S(1)} %bitcast.57), channel_id=1, source_target_pairs={{0,8},{8,16},{16,24},{1,9},{9,17},{17,25},{2,10},{10,18},{18,26},{... | collective-permute-start | bytes 602120 | tf_op jit(solution)/shard_map/ppermute | solution.py:14
  39.8 6.1 %collective-permute-done = bf16[98,1024]{1,0:T(8,128)(2,1)S(1)} collective-permute-done((bf16[98,1024]{1,0:T(8,128)(2,1)S(1)}, bf16[98,1024]{1,0:T(8,128)(2,1)S(1)}, u32[]{:S(2)}, u32[]{:S(2)}) %collective-permute-start) | collective-permute-done | bytes 200736 | tf_op jit(solution)/shard_map/ppermute | solution.py:14
  46.0 0.8 convert_reduce_fusion
  46.8 0.6 dynamic-slice.4
  48.0 16.0 %all-reduce.2 = (f32[1024]{0:T(1024)S(1)}, f32[1024]{0:T(1024)S(1)}) all-reduce(f32[1024]{0:T(1024)S(1)} %get-tuple-element.19, f32[1024]{0:T(1024)S(1)} %get-tuple-element.18), channel_id=1, replica_groups=mesh['section'=4,'dev'=8] {'dev'}, use_global_device_ids=true, to_apply=%region_1.2 | all-reduce | flops 2048 | bytes 16384 | tf_op jit(solution)/shard_map/psum | solution.py:46
  64.1 3.9 %fusion.5 = bf16[1,1568,256]{2,1,0:T(8,128)(2,1)} fusion(bf16[1568,256]{1,0:T(8,128)(2,1)S(1)} %broadcast_select_fusion, bf16[1568,1024]{1,0:T(8,128)(2,1)} %copy-done.14, bf16[1,256,1024]{2,1,0:T(8,128)(2,1)S(1)} %copy-done.4), kind=kOutput, calls=%fused_computation.15 | convolution fusion | flops 823287808 | bytes 5341184 | tf_op jit(solution)/shard_map/dot_general | solution.py:90
  67.9 36.3 %all-reduce.6.cloned.1.call-done = (f32[256,1024]{0,1:T(8,128)}, f32[1024,256]{1,0:T(8,128)}) async-done(((f32[256,1024]{0,1:T(8,128)}, f32[1024,256]{1,0:T(8,128)}), (f32[256,1024]{0,1:T(8,128)}, f32[1024,256]{1,0:T(8,128)})) %all-reduce.6.cloned.1.call-update) | async-done | bytes 2097168 | tf_op jit(solution)/shard_map/psum | solution.py:89
  104.2 1.4 multiply_bitcast_fusion.1
  105.6 28.3 %all-gather.3.cloned.1.call-done = bf16[8,98,1024]{2,1,0:T(8,128)(2,1)} async-done(((bf16[1,98,1024]{2,1,0:T(8,128)(2,1)}), bf16[8,98,1024]{2,1,0:T(8,128)(2,1)}) %all-gather.3.cloned.1.call-update) | async-done | bytes 1605648 | tf_op jit(solution)/shard_map/all_gather | solution.py:49
  133.9 3.0 %reshape.47 = f32[784,1024]{1,0:T(8,128)} reshape(bf16[8,98,1024]{2,1,0:T(8,128)(2,1)} %all-gather.3.cloned.1.call-done) | data formatting | bytes 4816896 | tf_op jit(solution)/shard_map/convert_element_type | solution.py:49
  136.9 3.1 %multiply_reduce_fusion = (f32[512]{0:T(512)S(1)}, f32[512]{0:T(512)S(1)}, f32[784,512]{1,0:T(8,128)S(1)}) fusion(bf16[1,1024,512]{2,1,0:T(8,128)(2,1)S(1)} %copy-done.11, f32[784,1024]{1,0:T(8,128)} %reshape.47, f32[1024]{0:T(1024)S(1)} %get-tuple-element.26, f32[1024]{0:T(1024)S(1)} %get-tuple-element.27), kind=kOutput, calls=%fused_computation.8 | convolution fusion | flops 828906496 | bytes 5877760 | tf_op jit(solution)/shard_map/dot_general | solution.py:51
  140.0 2.2 %convolution_convert_fusion = bf16[784,1024]{1,0:T(8,128)(2,1)} fusion(bf16[1,512,1024]{2,1,0:T(8,128)(2,1)S(1)} %copy-done, f32[784,512]{1,0:T(8,128)S(1)} %get-tuple-element.29, f32[512]{0:T(512)S(1)} %bitcast.54, f32[512]{0:T(512)S(1)} %bitcast.55), kind=kOutput, calls=%fused_computation.5 | convolution fusion | flops 825696256 | bytes 4263936 | tf_op jit(solution)/shard_map/dot_general | solution.py:62
  142.3 22.4 %fusion = bf16[104,1024]{1,0:T(8,128)(2,1)S(1)} fusion(bf16[784,1024]{1,0:T(8,128)(2,1)} %convolution_convert_fusion), kind=kCustom, calls=%all-reduce-scatter | all-reduce-scatter fusion | flops 851969 | bytes 1819136
  164.7 2.8 %collective-permute-start.2 = (bf16[42,1024]{1,0:T(8,128)(2,1)S(1)}, bf16[42,1024]{1,0:T(8,128)(2,1)S(1)}, u32[]{:S(2)}, u32[]{:S(2)}) collective-permute-start(bf16[42,1024]{1,0:T(8,128)(2,1)S(1)} %slice), channel_id=1, source_target_pairs={{0,1},{1,2},{2,3},{3,4},{4,5},{5,6},{6,7},{8,9},{9,10},{10,11},{11... | collective-permute-start | bytes 258056
  167.5 2.3 %multiply_bitcast_fusion = f32[1,1024,256]{2,1,0:T(8,128)} fusion(f32[1024,256]{1,0:T(8,128)} %get-tuple-element.23), kind=kLoop, calls=%fused_computation.13 | loop fusion | flops 262144 | bytes 2097152 | tf_op jit(solution)/shard_map/broadcast_in_dim | solution.py:97
  169.8 1.3 copy.19
  171.4 0.8 fusion.20
  (40 shorter events, 0.6 us)
Async XLA Ops:
  7.2 132.9 %copy-start = (bf16[1,512,1024]{2,1,0:T(8,128)(2,1)S(1)}, bf16[1,512,1024]{2,1,0:T(8,128)(2,1)}, u32[]{:S(2)}) copy-start(bf16[1,512,1024]{2,1,0:T(8,128)(2,1)} %param.20) | copy-start | bytes 3145732
  7.2 97.0 %all-reduce.6.cloned.1.call-start = ((), (), s32[]{:S(2)}) async-start(), calls=%async_computation.1 | async-start | bytes 4194304 | tf_op jit(solution)/shard_map/psum | solution.py:89
  7.2 21.0 %collective-permute-start.1 = (bf16[1568,256]{1,0:T(8,128)(2,1)}, bf16[1568,256]{1,0:T(8,128)(2,1)S(1)}, u32[]{:S(2)}, u32[]{:S(2)}) collective-permute-start(bf16[1568,256]{1,0:T(8,128)(2,1)} %bitcast.56), channel_id=1, source_target_pairs={{8,0},{16,8},{24,16},{9,1},{17,9},{25,17},{10,2},{18,10},{26,18},{... | collective-permute-start | bytes 2408456 | tf_op jit(solution)/shard_map/ppermute | solution.py:14
  10.4 17.8 %copy-start.3 = (bf16[1568,256]{1,0:T(8,128)(2,1)S(1)}, bf16[1568,256]{1,0:T(8,128)(2,1)}, u32[]{:S(2)}) copy-start(bf16[1568,256]{1,0:T(8,128)(2,1)} %param.23) | copy-start | bytes 2408452
  28.4 2.9 %copy-start.12 = (bf16[1,1024,256]{2,1,0:T(8,128)(2,1)S(1)}, bf16[1,1024,256]{2,1,0:T(8,128)(2,1)}, u32[]{:S(2)}) copy-start(bf16[1,1024,256]{2,1,0:T(8,128)(2,1)} %param.25) | copy-start | bytes 1572868
  31.2 4.4 %copy-start.2 = (bf16[1,1568,256]{2,1,0:T(8,128)(2,1)S(1)}, bf16[1,1568,256]{2,1,0:T(8,128)(2,1)}, u32[]{:S(2)}) copy-start(bf16[1,1568,256]{2,1,0:T(8,128)(2,1)} %param.21) | copy-start | bytes 2408452
  34.0 1.7 copy-start.14
  35.6 2.3 %copy-start.13 = (bf16[1,98,1024]{2,1,0:T(8,128)(2,1)S(1)}, bf16[1,98,1024]{2,1,0:T(8,128)(2,1)}, u32[]{:S(2)}) copy-start(bf16[1,98,1024]{2,1,0:T(8,128)(2,1)} %param.13) | copy-start | bytes 602116
  35.6 10.3 %copy-start.5 = (bf16[98,1024]{1,0:T(8,128)(2,1)S(1)}, bf16[98,1024]{1,0:T(8,128)(2,1)}, u32[]{:S(2)}) copy-start(bf16[98,1024]{1,0:T(8,128)(2,1)} %param.14) | copy-start | bytes 602116
  35.6 11.1 %copy-start.10 = (u32[32]{0:T(128)S(1)}, u32[32]{0:T(128)}, u32[]{:S(2)}) copy-start(u32[32]{0:T(128)} %constant.46) | copy-start | bytes 388
  35.6 28.4 %copy-start.6 = (f32[1,1024]{1,0:T(1,128)S(1)}, f32[1,1024]{1,0:T(1,128)}, u32[]{:S(2)}) copy-start(f32[1,1024]{1,0:T(1,128)} %param.16) | copy-start | bytes 12292
  35.6 28.4 %copy-start.7 = (f32[1,1024]{1,0:T(1,128)S(1)}, f32[1,1024]{1,0:T(1,128)}, u32[]{:S(2)}) copy-start(f32[1,1024]{1,0:T(1,128)} %param.15) | copy-start | bytes 12292
  35.7 28.4 %copy-start.4 = (bf16[1,256,1024]{2,1,0:T(8,128)(2,1)S(1)}, bf16[1,256,1024]{2,1,0:T(8,128)(2,1)}, u32[]{:S(2)}) copy-start(bf16[1,256,1024]{2,1,0:T(8,128)(2,1)} %param.24) | copy-start | bytes 1572868
  37.8 96.1 %all-gather.3.cloned.1.call-start = ((), (), s32[]{:S(2)}) async-start(), calls=%async_computation | async-start | bytes 1916928 | tf_op jit(solution)/shard_map/all_gather | solution.py:49
  37.9 8.1 %collective-permute-start = (bf16[98,1024]{1,0:T(8,128)(2,1)S(1)}, bf16[98,1024]{1,0:T(8,128)(2,1)S(1)}, u32[]{:S(2)}, u32[]{:S(2)}) collective-permute-start(bf16[98,1024]{1,0:T(8,128)(2,1)S(1)} %bitcast.57), channel_id=1, source_target_pairs={{0,8},{8,16},{16,24},{1,9},{9,17},{17,25},{2,10},{10,18},{18,26},{... | collective-permute-start | bytes 602120 | tf_op jit(solution)/shard_map/ppermute | solution.py:14
  104.2 32.7 %copy-start.11 = (bf16[1,1024,512]{2,1,0:T(8,128)(2,1)S(1)}, bf16[1,1024,512]{2,1,0:T(8,128)(2,1)}, u32[]{:S(2)}) copy-start(bf16[1,1024,512]{2,1,0:T(8,128)(2,1)} %param.17) | copy-start | bytes 3145732
  136.9 3.1 %copy-start.8 = (f32[1,512]{1,0:T(1,128)S(1)}, f32[1,512]{1,0:T(1,128)}, u32[]{:S(2)}) copy-start(f32[1,512]{1,0:T(1,128)} %param.19) | copy-start | bytes 6148
  136.9 3.1 %copy-start.9 = (f32[1,512]{1,0:T(1,128)S(1)}, f32[1,512]{1,0:T(1,128)}, u32[]{:S(2)}) copy-start(f32[1,512]{1,0:T(1,128)} %param.18) | copy-start | bytes 6148
  142.3 29.1 %copy-start.1 = (bf16[98,1024]{1,0:T(8,128)(2,1)S(1)}, bf16[98,1024]{1,0:T(8,128)(2,1)}, u32[]{:S(2)}) copy-start(bf16[98,1024]{1,0:T(8,128)(2,1)} %get-tuple-element.28) | copy-start | bytes 602116
  164.7 6.4 %collective-permute-start.2 = (bf16[42,1024]{1,0:T(8,128)(2,1)S(1)}, bf16[42,1024]{1,0:T(8,128)(2,1)S(1)}, u32[]{:S(2)}, u32[]{:S(2)}) collective-permute-start(bf16[42,1024]{1,0:T(8,128)(2,1)S(1)} %slice), channel_id=1, source_target_pairs={{0,1},{1,2},{2,3},{3,4},{4,5},{5,6},{6,7},{8,9},{9,10},{10,11},{11... | collective-permute-start | bytes 258056
Sparse Core Ops, SparseCore 0:
  37.9 66.2 all-reduce.5
  106.4 27.4 all-gather.2
where the time goes:
time: 183 us; the launch traced here: 179 us
  waiting for transfers between devices  86.1 us (47%)
  blocking collectives  38.4 us (21%)
  matrix products  19.2 us (10%)
  between operations  14.9 us (8%)
  starting transfers between devices  7.99 us (4%)
  local copies, waits for them, and re-layouts  6.93 us (4%)
  other arithmetic  5.38 us (3%)
    psum x1, waiting for transfers between devices, early_part(): summed_expand, summed_reduce = lax.psum((local_expand, local_reduce), 'dev')  36.3 us
    all_gather x1, waiting for transfers between devices, late_part(): lax.all_gather(own_rows, 'dev', axis=0, tiled=True).astype(jnp.float32)  28.3 us
    unnamed x1, blocking collectives  22.4 us
    ppermute x2, waiting for transfers between devices, from_behind(): return lax.ppermute(x, axis, pairs)  21.6 us
    psum x1, blocking collectives, late_part(): lax.psum((jnp.sum(values, axis=0), jnp.sum(values * values, axis=0)), 'dev')  16 us
    ppermute x2, starting transfers between devices, from_behind(): return lax.ppermute(x, axis, pairs)  5.11 us
    unnamed x34, local copies, waits for them, and re-layouts  3.93 us
    dot_general x1, matrix products, early_part(): lax.dot_general(slope, expand, (((1,), (1,)), ((), ())), preferred_elemen...  3.85 us
  transfers between devices with their start and end apart: 5, of which 4 were waited for; matrix products, arithmetic and copies ran while one was open for 7% of the time, Pallas kernels for 0%

commit v1 on v0

v1 whole, which is shorter than its diff:
```python
import functools
import math

import jax
import jax.numpy as jnp
from jax import lax
from jax.experimental import pallas as pl
from jax.experimental.pallas import tpu as pltpu
from jax.sharding import PartitionSpec as P

MESH = pl.DeviceIdType.MESH
epsilon = 1e-05
F32 = jnp.float32
BF16 = jnp.bfloat16


def sigmoid(x):
    return 0.5 * jnp.tanh(0.5 * x) + 0.5


def affine(sums, squares, count, gain, shift):
    average = sums / count
    second = squares / count
    spread = gain * lax.rsqrt(second - average * average + epsilon)
    return spread, shift - average * spread


def dot(a, b, ca=1, cb=0):
    return lax.dot_general(a, b, (((ca,), (cb,)), ((), ())), preferred_element_type=F32)


def kernel(
    sections, n_dev, chunk,
    late_hbm, entry_hbm, gain1, shift1, wexp_hbm, gain2, shift2, wred_hbm,
    saved_hbm, up_hbm, exit_hbm, eexp_hbm, ered_hbm,
    late_out, input_grad, wout,
    lbuf, first, hidden, part, prx, ltx, lrx,
    wexp, wred, saved, grad, eexp, ered, act, dsl, slope,
    gsum, gtx, gprx, wtx, wrx, abuf,
    loc_sem, perm_send, perm_recv, gp_send, gp_recv,
    ag_s, ag_r, agp_s, agp_r, px_s, px_r, rs_s, rs_r,
    gx_s, gx_r, wrs_s, wrs_r, wag_s, wag_r, wagp_s, wagp_r,
):
    Q = n_dev // 2
    s = lax.axis_index("section")
    d = lax.axis_index("dev")
    q = d // 2
    c = lax.rem(d, 2)
    other = 1 - c
    partner = q * 2 + other
    rows = late_hbm.shape[0]
    half = late_hbm.shape[1] // 2
    padded = first.shape[0] // n_dev
    e_rows = saved_hbm.shape[0]
    steps = e_rows // chunk
    total_rows = rows * n_dev
    hid = wexp.shape[1]

    def at_chip(offset):
        return lax.rem(q + offset + 2 * Q, Q)

    sgn = (1, -1)
    nxt = tuple(at_chip(g) * 2 + c for g in sgn)

    barrier = pltpu.get_barrier_semaphore()
    for dev in (nxt[0], nxt[1], partner):
        pl.semaphore_signal(barrier, inc=1, device_id=(s, dev), device_id_type=MESH)

    @pl.when(s > 0)
    def _():
        pl.semaphore_signal(barrier, inc=1, device_id=(s - 1, d), device_id_type=MESH)

    @pl.when(s < sections - 1)
    def _():
        pl.semaphore_signal(barrier, inc=1, device_id=(s + 1, d), device_id_type=MESH)

    local = [
        pltpu.make_async_copy(src, dst, loc_sem.at[i])
        for i, (src, dst) in enumerate(
            ((saved_hbm, saved), (eexp_hbm, eexp), (ered_hbm, ered), (wexp_hbm, wexp), (wred_hbm, wred))
        )
    ]
    for copy in local:
        copy.start()

    pl.semaphore_wait(barrier, 3 + jnp.minimum(s, 1) + jnp.minimum(sections - 1 - s, 1))

    def remote(src, dst, send, recv, section, dev):
        return pltpu.make_async_remote_copy(
            src_ref=src, dst_ref=dst, send_sem=send, recv_sem=recv,
            device_id=(section, dev), device_id_type=MESH,
        )

    def cols(h):
        return pl.ds(h * half, half)

    def late_copy(h):
        return remote(
            late_hbm.at[:, cols(h)], lbuf.at[h, d], perm_send.at[h], perm_recv.at[h],
            jnp.minimum(s + 1, sections - 1), d,
        )

    def entry_copy(h):
        return pltpu.make_async_copy(entry_hbm.at[:, cols(h)], lbuf.at[h, d], perm_recv.at[h])

    def chunk_rows(j):
        return pl.ds(j * chunk, chunk)

    def grad_copy(j):
        return remote(
            up_hbm.at[chunk_rows(j)], grad.at[chunk_rows(j)], gp_send.at[j], gp_recv.at[j],
            jnp.maximum(s - 1, 0), d,
        )

    def exit_copy(j):
        return pltpu.make_async_copy(exit_hbm.at[chunk_rows(j)], grad.at[chunk_rows(j)], gp_recv.at[j])

    @pl.when(s < sections - 1)
    def _():
        for h in range(2):
            late_copy(h).start()

    @pl.when(s == 0)
    def _():
        for h in range(2):
            entry_copy(h).start()

    @pl.when(s > 0)
    def _():
        for j in range(steps):
            grad_copy(j).start()

    @pl.when(s == sections - 1)
    def _():
        for j in range(steps):
            exit_copy(j).start()

    def ring_gather(buf, ss, rr, ps, pr):
        def owner(h, t, lane):
            return at_chip(-sgn[h] * t) * 2 + lane

        def hop(h, t):
            piece = buf.at[h, owner(h, t, c)]
            return remote(piece, piece, ss.at[h, t], rr.at[h, t], s, nxt[h])

        def arrival(h, t):
            piece = buf.at[h, owner(h, t + 1, c)]
            return remote(piece, piece, ss.at[h, t], rr.at[h, t], s, nxt[h])

        def share(h, t, lane):
            piece = buf.at[h, owner(h, t, lane)]
            return remote(piece, piece, ps.at[h, t], pr.at[h, t], s, partner)

        def start(h):
            hop(h, 0).start()
            share(h, 0, c).start()

        def advance(h, t):
            arrival(h, t).wait_recv()
            if t + 1 < Q - 1:
                hop(h, t + 1).start()
            share(h, t + 1, c).start()

        def finish():
            for h in range(2):
                for t in range(Q):
                    share(h, t, other).wait_recv()

        def drain():
            for h in range(2):
                for t in range(Q - 1):
                    hop(h, t).wait_send()
                for t in range(Q):
                    share(h, t, c).wait_send()

        return start, advance, finish, drain

    def ring_scatter(mine, tx, rx, ss, rr):
        def hop(h, t):
            return remote(tx.at[h, t], rx.at[h, t], ss.at[h, t], rr.at[h, t], s, nxt[h])

        def start(h):
            tx[h, 0] = mine(h, at_chip(-sgn[h])).astype(BF16)
            hop(h, 0).start()

        def advance(h, t):
            hop(h, t).wait_recv()
            value = mine(h, at_chip(-sgn[h] * (t + 2))) + rx[h, t].astype(F32)
            if t == Q - 2:
                return value
            tx[h, t + 1] = value.astype(BF16)
            hop(h, t + 1).start()

        def drain():
            for h in range(2):
                for t in range(Q - 1):
                    hop(h, t).wait_send()

        return start, advance, drain

    def forward(j):
        at = chunk_rows(j)
        pre = dot(saved[at], eexp[...])
        sigma = sigmoid(pre)
        value = pre * sigma
        act[at] = value.astype(BF16)
        dsl[at] = sigma * (1.0 + pre - value)

    def backward(j):
        at = chunk_rows(j)

        @pl.when(s < sections - 1)
        def _():
            grad_copy(j).wait_recv()

        @pl.when(s == sections - 1)
        def _():
            exit_copy(j).wait()

        g = grad[at]
        back = dot(g, ered[...], 1, 1)
        sl = (back * dsl[at]).astype(BF16)
        slope[at] = sl
        input_grad[at] = (g.astype(F32) + dot(sl, eexp[...], 1, 1)).astype(BF16)

    local[0].wait()
    local[1].wait()
    fwd = 0
    first_part = max(steps // 2, 1)
    for j in range(first_part):
        forward(j)
    fwd = first_part

    @pl.when(s == 0)
    def _():
        for h in range(2):
            entry_copy(h).wait()

    @pl.when(s > 0)
    def _():
        for h in range(2):
            late_copy(h).wait_recv()

    ag_start, ag_advance, ag_finish, ag_drain = ring_gather(lbuf, ag_s, ag_r, agp_s, agp_r)
    for h in range(2):
        ag_start(h)
    for dev in range(n_dev):
        first[pl.ds((dev + 1) * padded - 16, 16), :] = jnp.zeros((16, first.shape[1]), BF16)
    for t in range(Q - 1):
        if fwd < steps:
            forward(fwd)
            fwd += 1
        for h in range(2):
            ag_advance(h, t)
    for j in range(fwd, steps):
        forward(j)
    ag_finish()

    for h in range(2):
        total = jnp.zeros((1, half), F32)
        squares = jnp.zeros((1, half), F32)
        for dev in range(n_dev):
            v = lbuf[h, dev].astype(F32)
            total += jnp.sum(v, axis=0, keepdims=True)
            squares += jnp.sum(v * v, axis=0, keepdims=True)
        spread, offset = affine(total, squares, total_rows, gain1[:, cols(h)], shift1[:, cols(h)])
        for dev in range(n_dev):
            v = lbuf[h, dev].astype(F32) * spread + offset
            first[pl.ds(dev * padded, rows), cols(h)] = (v * sigmoid(v)).astype(BF16)

    local[3].wait()
    local[4].wait()
    width = min(256, hid)
    for n in range(hid // width):
        at = pl.ds(n * width, width)
        inner = dot(first[...], wexp[:, at])
        spread, offset = affine(
            jnp.sum(inner, axis=0, keepdims=True),
            jnp.sum(inner * inner, axis=0, keepdims=True),
            total_rows, gain2[:, at], shift2[:, at],
        )
        v = inner * spread + offset
        hidden[:, at] = (v * sigmoid(v)).astype(BF16)

    def pair_copy(h):
        return remote(part.at[other, h], prx.at[h], px_s.at[h], px_r.at[h], s, partner)

    tile = min(256, half)
    for h in range(2):
        for n in range(half // tile):
            value = dot(hidden[...], wred[:, pl.ds(h * half + n * tile, tile)]).astype(BF16)
            for dev in range(n_dev):
                part[dev % 2, h, dev // 2, :, pl.ds(n * tile, tile)] = value[dev * padded:dev * padded + rows]
        pair_copy(h).start()

    def late_term(h, k):
        return part[c, h, k].astype(F32) + prx[h, k].astype(F32)

    rs_start, rs_advance, rs_drain = ring_scatter(late_term, ltx, lrx, rs_s, rs_r)
    for h in range(2):
        pair_copy(h).wait_recv()
        rs_start(h)

    local[2].wait()
    bwd = 0
    per = -(-steps // (Q - 1))
    for t in range(Q - 1):
        for j in range(bwd, min(bwd + per, steps)):
            backward(j)
        bwd = min(bwd + per, steps)
        for h in range(2):
            value = rs_advance(h, t)
            if t == Q - 2:
                late_out[:, cols(h)] = (lbuf[h, d].astype(F32) + value).astype(BF16)

    depth = gsum.shape[2]
    wide = eexp.shape[1]
    for n in range(wide // 256):
        at = pl.ds(n * 256, 256)
        gsum[0, :, :, at] = dot(saved[...], slope[:, at], 0, 0).reshape(Q, depth, 256)
        gsum[1, :, :, at] = dot(grad[...], act[:, at], 0, 0).reshape(Q, depth, 256)
    gtx[...] = gsum[other].astype(BF16)
    gx = remote(gtx, gprx, gx_s, gx_r, s, partner)
    gx.start()
    gx.wait_recv()
    whalf = wide // 2

    def wcols(h):
        return pl.ds(h * whalf, whalf)

    def weight_term(h, k):
        return gsum[c, k, :, wcols(h)] + gprx[k, :, wcols(h)].astype(F32)

    ws_start, ws_advance, ws_drain = ring_scatter(weight_term, wtx, wrx, wrs_s, wrs_r)
    wg_start, wg_advance, wg_finish, wg_drain = ring_gather(abuf, wag_s, wag_r, wagp_s, wagp_r)
    factor = 1.0 / math.sqrt(e_rows * n_dev)
    for h in range(2):
        ws_start(h)
    for t in range(Q - 1):
        for h in range(2):
            value = ws_advance(h, t)
            if t == Q - 2:
                abuf[h, d] = (value * factor).astype(BF16)
                wg_start(h)
    for t in range(Q - 1):
        for h in range(2):
            wg_advance(h, t)
    wg_finish()
    for h in range(2):
        for k in range(Q):
            for lane in range(2):
                wout[lane, k, :, wcols(h)] = abuf[h, 2 * k + lane].astype(F32)

    @pl.when(s < sections - 1)
    def _():
        for h in range(2):
            late_copy(h).wait_send()

    @pl.when(s > 0)
    def _():
        for j in range(steps):
            grad_copy(j).wait_send()

    ag_drain()
    for h in range(2):
        pair_copy(h).wait_send()
    rs_drain()
    gx.wait_send()
    ws_drain()
    wg_drain()


def shards(
    sections, n_dev,
    late_sent, entry_rows, gain_first, shift_first, expand_late, gain_inner, shift_inner,
    reduce_late, early_saved, upstream_grad, exit_grad, expand_early, reduce_early,
):
    rows, cl = entry_rows.shape
    e_rows, ce = exit_grad.shape
    fe = expand_early.shape[2]
    hid = expand_late.shape[2]
    Q = n_dev // 2
    half = cl // 2
    padded = -(-rows // 16) * 16
    chunk = max(k for k in range(16, 257, 16) if e_rows % k == 0)
    steps = e_rows // chunk
    depth = ce // Q
    any_spec = pl.BlockSpec(memory_space=pl.ANY)
    vm = pl.BlockSpec(memory_space=pltpu.VMEM)
    V = pltpu.VMEM
    dma = pltpu.SemaphoreType.DMA
    ring = [dma((2, Q - 1)), dma((2, Q - 1))]
    late_out, input_grad, wout = pl.pallas_call(
        functools.partial(kernel, sections, n_dev, chunk),
        out_shape=(
            jax.ShapeDtypeStruct((rows, cl), BF16),
            jax.ShapeDtypeStruct((e_rows, ce), BF16),
            jax.ShapeDtypeStruct((2, Q, depth, fe), F32),
        ),
        in_specs=[any_spec, any_spec, vm, vm, any_spec, vm, vm] + [any_spec] * 6,
        out_specs=(vm, vm, vm),
        scratch_shapes=[
            V((2, n_dev, rows, half), BF16),
            V((n_dev * padded, cl), BF16),
            V((n_dev * padded, hid), BF16),
            V((2, 2, Q, rows, half), BF16),
            V((2, Q, rows, half), BF16),
            V((2, Q - 1, rows, half), BF16),
            V((2, Q - 1, rows, half), BF16),
            V((cl, hid), BF16),
            V((hid, cl), BF16),
            V((e_rows, ce), BF16),
            V((e_rows, ce), BF16),
            V((ce, fe), BF16),
            V((fe, ce), BF16),
            V((e_rows, fe), BF16),
            V((e_rows, fe), F32),
            V((e_rows, fe), BF16),
            V((2, Q, depth, fe), F32),
            V((Q, depth, fe), BF16),
            V((Q, depth, fe), BF16),
            V((2, Q - 1, depth, fe // 2), BF16),
            V((2, Q - 1, depth, fe // 2), BF16),
            V((2, n_dev, depth, fe // 2), BF16),
            dma((5,)), dma((2,)), dma((2,)), dma((steps,)), dma((steps,)),
            *ring, dma((2, Q)), dma((2, Q)), dma((2,)), dma((2,)), *ring,
            dma, dma, *ring, *ring, dma((2, Q)), dma((2, Q)),
        ],
        compiler_params=pltpu.CompilerParams(
            collective_id=0, has_side_effects=True, vmem_limit_bytes=60 * 1024 * 1024
        ),
        name="relay",
    )(
        late_sent[0], entry_rows, gain_first, shift_first, expand_late[0], gain_inner, shift_inner,
        reduce_late[0], early_saved[0], upstream_grad[0], exit_grad, expand_early[0], reduce_early[0],
    )
    wout = wout.reshape(2, ce, fe)
    return late_out[None], input_grad[None], wout[0][None], wout[1].T[None]


def solution(mesh):
    sections, n_dev = mesh.shape["section"], mesh.shape["dev"]
    sd, dd = P("section", "dev", None), P("dev", None)
    rep, one = P("section", None, None), P("section", None)
    in_specs = (
        sd, dd, one, one, P("section", None, "dev"), P("section", "dev"), P("section", "dev"),
        sd, sd, sd, dd, rep, rep,
    )
    return jax.shard_map(
        functools.partial(shards, sections, n_dev), mesh=mesh, in_specs=in_specs,
        out_specs=(sd, sd, rep, rep), check_vma=False,
    )
```

time: 183 us -> 92.3 us (0.50)
  the two profiles are of different devices: /device:TPU:5 before, /device:TPU:31 now
where the time goes in v1:
time: 92.3 us; the launch traced here: 92.1 us
  Pallas kernels  85.8 us (93%)
  local copies, waits for them, and re-layouts  5.59 us (6%)
    pallas_call x1, Pallas kernels, shards(): pl.pallas_call(functools.partial(kernel, sections, n_dev, chunk), out_sha...  85.8 us
    slice x1, local copies, waits for them, and re-layouts, shards(): return (late_out[None], input_grad[None], wout[0][None], wout[1].T[None])  2.7 us

profile of v1, /device:TPU:31, one launch (start us, length us, event | category | flops | bytes accessed | tf_op | source)
XLA Modules:
  0.0 92.1 jit_solution(5116072458289069351)
XLA Ops:
  0.6 85.8 %relay.1 = (bf16[98,1024]{1,0:T(8,128)(2,1)}, bf16[1568,256]{1,0:T(8,128)(2,1)}, f32[2,4,64,1024]{3,2,1,0:T(8,128)}) custom-call(bf16[98,1024]{1,0:T(8,128)(2,1)} %bitcast.25, bf16[98,1024]{1,0:T(8,128)(2,1)} %entry_hbm.1, f32[1,1024]{1,0:T(1,128)} %gain1.1, f32[1,1024]{1,0:T(1,128)} %shift1.1, bf16[1024,512]{1,0:T(8,128)(2,1)} %bitcast.15, f32[1,512]{1,0:T(1,128)} %gain2.1, ...), custom_call_target="tpu_custom_call" | custom-call | tf_op jit(solution)/shard_map/relay/pallas_call | solution.py:393
  86.5 2.7 %fusion = (f32[1,4,64,1024]{3,2,1,0:T(8,128)S(1)}, f32[1,4,64,1024]{3,2,1,0:T(8,128)}) fusion(f32[2,4,64,1024]{3,2,1,0:T(8,128)} %get-tuple-element.9), kind=kLoop, calls=%fused_computation | loop fusion | bytes 4194304 | tf_op jit(solution)/shard_map/slice | solution.py:438
  89.2 0.0 copy-start.1
  89.2 0.0 copy-start
  89.2 1.3 %copy.17 = f32[256,1024]{0,1:T(8,128)} copy(f32[256,1024]{1,0:T(8,128)S(1)} %bitcast.14) | data formatting | bytes 2097152 | tf_op jit(solution)/shard_map/squeeze | solution.py:438
  90.5 0.0 copy-done.1
  90.5 0.7 copy.20
  91.2 0.0 copy-done
  91.2 0.9 copy.21
Async XLA Ops:
  89.2 1.3 %copy-start.1 = (bf16[98,1024]{1,0:T(8,128)(2,1)S(1)}, bf16[98,1024]{1,0:T(8,128)(2,1)}, u32[]{:S(2)}) copy-start(bf16[98,1024]{1,0:T(8,128)(2,1)} %get-tuple-element.7) | copy-start | bytes 602116
  89.2 2.0 %copy-start = (bf16[1568,256]{1,0:T(8,128)(2,1)S(1)}, bf16[1568,256]{1,0:T(8,128)(2,1)}, u32[]{:S(2)}) copy-start(bf16[1568,256]{1,0:T(8,128)(2,1)} %get-tuple-element.8) | copy-start | bytes 2408452

commit v2 on v1

--- a/solution.py
+++ b/solution.py
@@ -33,10 +33,10 @@
     sections, n_dev, chunk,
     late_hbm, entry_hbm, gain1, shift1, wexp_hbm, gain2, shift2, wred_hbm,
     saved_hbm, up_hbm, exit_hbm, eexp_hbm, ered_hbm,
-    late_out, input_grad, wout,
+    late_out, input_grad, gexp_out, gred_out,
     lbuf, first, hidden, part, prx, ltx, lrx,
     wexp, wred, saved, grad, eexp, ered, act, dsl, slope,
-    gsum, gtx, gprx, wtx, wrx, abuf,
+    gsum, gtx, gprx, wtx, wrx, abuf, turn,
     loc_sem, perm_send, perm_recv, gp_send, gp_recv,
     ag_s, ag_r, agp_s, agp_r, px_s, px_r, rs_s, rs_r,
     gx_s, gx_r, wrs_s, wrs_r, wag_s, wag_r, wagp_s, wagp_r,
@@ -250,10 +250,25 @@
         if fwd < steps:
             forward(fwd)
             fwd += 1
+        if t == Q - 2:
+            for j in range(fwd, steps):
+                forward(j)
+            fwd = steps
         for h in range(2):
             ag_advance(h, t)
-    for j in range(fwd, steps):
-        forward(j)
+
+    local[2].wait()
+    for j in range(steps):
+        backward(j)
+    depth = gsum.shape[2]
+    wide = eexp.shape[1]
+    for n in range(wide // 256):
+        at = pl.ds(n * 256, 256)
+        gsum[0, :, :, at] = dot(saved[...], slope[:, at], 0, 0).reshape(Q, depth, 256)
+        gsum[1, :, :, at] = dot(grad[...], act[:, at], 0, 0).reshape(Q, depth, 256)
+    gtx[...] = gsum[other].astype(BF16)
+    gx = remote(gtx, gprx, gx_s, gx_r, s, partner)
+    gx.start()
     ag_finish()
 
     for h in range(2):
@@ -267,6 +282,29 @@
         for dev in range(n_dev):
             v = lbuf[h, dev].astype(F32) * spread + offset
             first[pl.ds(dev * padded, rows), cols(h)] = (v * sigmoid(v)).astype(BF16)
+
+    gx.wait_recv()
+    whalf = wide // 2
+
+    def wcols(h):
+        return pl.ds(h * whalf, whalf)
+
+    def weight_term(h, k):
+        return gsum[c, k, :, wcols(h)] + gprx[k, :, wcols(h)].astype(F32)
+
+    ws_start, ws_advance, ws_drain = ring_scatter(weight_term, wtx, wrx, wrs_s, wrs_r)
+    wg_start, wg_advance, wg_finish, wg_drain = ring_gather(abuf, wag_s, wag_r, wagp_s, wagp_r)
+    factor = 1.0 / math.sqrt(e_rows * n_dev)
+
+    def weight_step(t):
+        for h in range(2):
+            value = ws_advance(h, t)
+            if t == Q - 2:
+                abuf[h, d] = (value * factor).astype(BF16)
+                wg_start(h)
+
+    for h in range(2):
+        ws_start(h)
 
     local[3].wait()
     local[4].wait()
@@ -293,6 +331,8 @@
                 part[dev % 2, h, dev // 2, :, pl.ds(n * tile, tile)] = value[dev * padded:dev * padded + rows]
         pair_copy(h).start()
 
+    weight_step(0)
+
     def late_term(h, k):
         return part[c, h, k].astype(F32) + prx[h, k].astype(F32)
 
@@ -301,55 +341,24 @@
         pair_copy(h).wait_recv()
         rs_start(h)
 
-    local[2].wait()
-    bwd = 0
-    per = -(-steps // (Q - 1))
+    for t in range(1, Q - 1):
+        weight_step(t)
     for t in range(Q - 1):
-        for j in range(bwd, min(bwd + per, steps)):
-            backward(j)
-        bwd = min(bwd + per, steps)
         for h in range(2):
             value = rs_advance(h, t)
             if t == Q - 2:
                 late_out[:, cols(h)] = (lbuf[h, d].astype(F32) + value).astype(BF16)
-
-    depth = gsum.shape[2]
-    wide = eexp.shape[1]
+        for h in range(2):
+            wg_advance(h, t)
+    wg_finish()
+    for h in range(2):
+        for k in range(Q):
+            at = pl.ds(k * depth, depth)
+            gexp_out[at, wcols(h)] = abuf[h, 2 * k]
+            turn[at, wcols(h)] = abuf[h, 2 * k + 1].astype(F32)
     for n in range(wide // 256):
         at = pl.ds(n * 256, 256)
-        gsum[0, :, :, at] = dot(saved[...], slope[:, at], 0, 0).reshape(Q, depth, 256)
-        gsum[1, :, :, at] = dot(grad[...], act[:, at], 0, 0).reshape(Q, depth, 256)
-    gtx[...] = gsum[other].astype(BF16)
-    gx = remote(gtx, gprx, gx_s, gx_r, s, partner)
-    gx.start()
-    gx.wait_recv()
-    whalf = wide // 2
-
-    def wcols(h):
-        return pl.ds(h * whalf, whalf)
-
-    def weight_term(h, k):
-        return gsum[c, k, :, wcols(h)] + gprx[k, :, wcols(h)].astype(F32)
-
-    ws_start, ws_advance, ws_drain = ring_scatter(weight_term, wtx, wrx, wrs_s, wrs_r)
-    wg_start, wg_advance, wg_finish, wg_drain = ring_gather(abuf, wag_s, wag_r, wagp_s, wagp_r)
-    factor = 1.0 / math.sqrt(e_rows * n_dev)
-    for h in range(2):
-        ws_start(h)
-    for t in range(Q - 1):
-        for h in range(2):
-            value = ws_advance(h, t)
-            if t == Q - 2:
-                abuf[h, d] = (value * factor).astype(BF16)
-                wg_start(h)
-    for t in range(Q - 1):
-        for h in range(2):
-            wg_advance(h, t)
-    wg_finish()
-    for h in range(2):
-        for k in range(Q):
-            for lane in range(2):
-                wout[lane, k, :, wcols(h)] = abuf[h, 2 * k + lane].astype(F32)
+        gred_out[at, :] = turn[:, at].T.astype(BF16)
 
     @pl.when(s < sections - 1)
     def _():
@@ -390,15 +399,16 @@
     V = pltpu.VMEM
     dma = pltpu.SemaphoreType.DMA
     ring = [dma((2, Q - 1)), dma((2, Q - 1))]
-    late_out, input_grad, wout = pl.pallas_call(
+    late_out, input_grad, gexp, gred = pl.pallas_call(
         functools.partial(kernel, sections, n_dev, chunk),
         out_shape=(
             jax.ShapeDtypeStruct((rows, cl), BF16),
             jax.ShapeDtypeStruct((e_rows, ce), BF16),
-            jax.ShapeDtypeStruct((2, Q, depth, fe), F32),
+            jax.ShapeDtypeStruct((ce, fe), BF16),
+            jax.ShapeDtypeStruct((fe, ce), BF16),
         ),
         in_specs=[any_spec, any_spec, vm, vm, any_spec, vm, vm] + [any_spec] * 6,
-        out_specs=(vm, vm, vm),
+        out_specs=(vm, vm, vm, vm),
         scratch_shapes=[
             V((2, n_dev, rows, half), BF16),
             V((n_dev * padded, cl), BF16),
@@ -422,6 +432,7 @@
             V((2, Q - 1, depth, fe // 2), BF16),
             V((2, Q - 1, depth, fe // 2), BF16),
             V((2, n_dev, depth, fe // 2), BF16),
+            V((ce, fe), F32),
             dma((5,)), dma((2,)), dma((2,)), dma((steps,)), dma((steps,)),
             *ring, dma((2, Q)), dma((2, Q)), dma((2,)), dma((2,)), *ring,
             dma, dma, *ring, *ring, dma((2, Q)), dma((2, Q)),
@@ -434,8 +445,7 @@
         late_sent[0], entry_rows, gain_first, shift_first, expand_late[0], gain_inner, shift_inner,
         reduce_late[0], early_saved[0], upstream_grad[0], exit_grad, expand_early[0], reduce_early[0],
     )
-    wout = wout.reshape(2, ce, fe)
-    return late_out[None], input_grad[None], wout[0][None], wout[1].T[None]
+    return late_out[None], input_grad[None], gexp.astype(F32)[None], gred.astype(F32)[None]
 
 
 def solution(mesh):

time: 92.3 us -> 81 us (0.88)
  the two profiles are of different devices: /device:TPU:31 before, /device:TPU:5 now
where the time goes in v2:
time: 81 us; the launch traced here: 80.8 us
  Pallas kernels  75.3 us (93%)
  other arithmetic  3.23 us (4%)
  local copies, waits for them, and re-layouts  1.58 us (2%)
    pallas_call x1, Pallas kernels, shards(): pl.pallas_call(functools.partial(kernel, sections, n_dev, chunk), out_sha...  75.3 us
    broadcast_in_dim x1, other arithmetic, shards(): gexp.astype(F32)[None]  2.18 us

profile of v2, /device:TPU:5, one launch (start us, length us, event | category | flops | bytes accessed | tf_op | source)
XLA Modules:
  0.0 80.8 jit_solution(10128425733560066309)
XLA Ops:
  0.6 75.3 %relay.1 = (bf16[98,1024]{1,0:T(8,128)(2,1)}, bf16[1568,256]{1,0:T(8,128)(2,1)}, bf16[256,1024]{1,0:T(8,128)(2,1)}, bf16[1024,256]{1,0:T(8,128)(2,1)}) custom-call(bf16[98,1024]{1,0:T(8,128)(2,1)} %bitcast.23, bf16[98,1024]{1,0:T(8,128)(2,1)} %entry_hbm.1, f32[1,1024]{1,0:T(1,128)} %gain1.1, f32[1,1024]{1,0:T(1,128)} %shift1.1, bf16[1024,512]{1,0:T(8,128)(2,1)} %bitcast.15, ...), custom_call_target="tpu_custom_call" | custom-call | tf_op jit(solution)/shard_map/relay/pallas_call | solution.py:402
  76.0 0.0 copy-start.1
  76.0 2.2 %bitcast_convert_fusion.1 = f32[1,256,1024]{2,1,0:T(8,128)} fusion(bf16[256,1024]{1,0:T(8,128)(2,1)} %get-tuple-element.10), kind=kLoop, calls=%fused_computation.1 | loop fusion | flops 262144 | bytes 1572864 | tf_op jit(solution)/shard_map/broadcast_in_dim | solution.py:448
  78.2 0.0 copy-done.1
  78.2 0.0 copy-start.2
  78.2 0.0 copy-start
  78.2 1.0 %bitcast_convert_fusion = f32[1,1024,256]{2,1,0:T(8,128)} fusion(bf16[1024,256]{1,0:T(8,128)(2,1)S(1)} %copy-done.1), kind=kLoop, calls=%fused_computation | loop fusion | flops 262144 | bytes 1572864 | tf_op jit(solution)/shard_map/broadcast_in_dim | solution.py:448
  79.2 0.0 copy-done.2
  79.2 0.7 copy.19
  79.9 0.0 copy-done
  79.9 0.9 %copy.20 = bf16[1,1568,256]{2,1,0:T(8,128)(2,1)} copy(bf16[1,1568,256]{2,1,0:T(8,128)(2,1)S(1)} %bitcast.19) | data formatting | bytes 1605632
Async XLA Ops:
  76.0 2.2 %copy-start.1 = (bf16[1024,256]{1,0:T(8,128)(2,1)S(1)}, bf16[1024,256]{1,0:T(8,128)(2,1)}, u32[]{:S(2)}) copy-start(bf16[1024,256]{1,0:T(8,128)(2,1)} %get-tuple-element.11) | copy-start | bytes 1572868
  78.2 1.1 %copy-start.2 = (bf16[98,1024]{1,0:T(8,128)(2,1)S(1)}, bf16[98,1024]{1,0:T(8,128)(2,1)}, u32[]{:S(2)}) copy-start(bf16[98,1024]{1,0:T(8,128)(2,1)} %get-tuple-element.8) | copy-start | bytes 602116
  78.2 1.7 %copy-start = (bf16[1568,256]{1,0:T(8,128)(2,1)S(1)}, bf16[1568,256]{1,0:T(8,128)(2,1)}, u32[]{:S(2)}) copy-start(bf16[1568,256]{1,0:T(8,128)(2,1)} %get-tuple-element.9) | copy-start | bytes 2408452
